TPU v7x, 32 devices: a whole 2x2x4 slice. The times are simulated.
32 devices in a mesh: blk: 8 (over z, y), layer: 4 (over x, core).
Axes of the slice: x: 2, y: 2, z: 4, core: 2. Of those that a mesh axis runs over, the one named last changes fastest.
Arguments:
- leaf_area: float32 [12, 16, 1024], P(None, 'layer', 'blk'), may hold values from 0 to 6
- soil_water: float32 [10, 1024], P(None, 'blk'), may hold values from 0.05 to 0.5
- root_share: float32 [16, 10], P('layer'), may hold values from 0 to 0.3
- patch_weight: float32 [16, 32768], P('layer', 'blk'), may hold values from 0 to 1
- patch_owner: int32 [32768, 1], P('blk'), may hold values from 0 to 7; in each aligned block of 4096 rows (0 to 4095, 4096 to 8191, ...) at most 1024 rows name the same one
- patch_local: int32 [32768], P('blk'), may hold values from 0 to 127
- month: int32 [1], replicated, may hold values from 0 to 11
- mix: float32 [1], replicated, may hold values from 0.1 to 0.9
Outputs:
- canopy_share: float32 [16, 1024], P('layer', 'blk')
Inputs may be any that keep to these rules, and one draw needn't show every extreme that they name: `patch_owner`: among the rows of one device, no owner is named more than 1024 times, a bound that some block reaches.
All inputs are finite; a program needn't handle non-finite values.
Results may differ from a plain program's by a relative error of at most 0.000065.
Values sent between devices are 32-bit elements; how exact they have to be, the bound alone decides.
A program may use at most 64 MiB of HBM per device.

v0:
```python
import jax
import jax.numpy as jnp
from jax import lax
from jax.sharding import PartitionSpec as P


def interpolate(leaf_area, month, mix):
    earlier_index = month[0]
    second = (earlier_index + 1) % leaf_area.shape[0]
    earlier = lax.dynamic_index_in_dim(leaf_area, earlier_index, 0, keepdims=False)
    later = lax.dynamic_index_in_dim(leaf_area, second, 0, keepdims=False)
    return mix[0] * earlier + (1.0 - mix[0]) * later


def canopy_terms(patch_weight, patch_leaf, patch_soil, root_share):
    stress = jnp.dot(root_share, patch_soil, precision=lax.Precision.HIGHEST)
    return patch_weight * (1.0 - jnp.exp(-0.5 * patch_leaf)) * stress


def exact_dot(left, right):
    return jnp.dot(left, right, precision=lax.Precision.HIGHEST)


def on_device(
    leaf_area, soil_water, root_share, patch_weight, patch_owner, patch_local, month, mix
):
    months_count, types_here, cells_here = leaf_area.shape
    patch_count = patch_local.shape[0]
    owners = patch_owner[:, 0]
    cell_iota = jnp.arange(cells_here, dtype=jnp.int32)
    devices = lax.axis_size("blk")
    capacity = max(2, 2 * patch_count // devices)
    owner_table = (owners[:, None] == jnp.arange(devices, dtype=jnp.int32)[None, :]).astype(
        jnp.float32
    )
    patch_iota = jnp.arange(patch_count, dtype=jnp.int32)
    earlier = (patch_iota[:, None] > patch_iota[None, :]).astype(jnp.float32)
    before = exact_dot(earlier, owner_table)
    ranks = jnp.sum(before * owner_table, axis=1).astype(jnp.int32)
    slots = owners * capacity + ranks
    slot_iota = jnp.arange(devices * capacity, dtype=jnp.int32)
    slot_table = (slots[:, None] == slot_iota[None, :]).astype(jnp.float32)
    packed = jnp.concatenate([patch_weight, patch_local.astype(jnp.float32)[None, :]], axis=0)
    buffer = exact_dot(packed, slot_table)
    received = lax.all_to_all(buffer, "blk", split_axis=1, concat_axis=1, tiled=True)
    weights = received[:types_here]
    cell_ids = received[types_here].astype(jnp.int32)
    cell_table = (cell_iota[:, None] == cell_ids[None, :]).astype(jnp.float32)
    current = interpolate(leaf_area, month, mix)
    patch_leaf = exact_dot(current, cell_table)
    patch_soil = exact_dot(soil_water, cell_table)
    canopy = canopy_terms(weights, patch_leaf, patch_soil, root_share)
    grid_sum = exact_dot(canopy, cell_table.T)
    total = lax.psum(jnp.sum(grid_sum, axis=0), "layer")
    return grid_sum / (1.0 + total)


def solution(mesh):
    in_specs = (
        P(None, "layer", "blk"),
        P(None, "blk"),
        P("layer", None),
        P("layer", "blk"),
        P("blk", None),
        P("blk"),
        P(),
        P(),
    )
    out_specs = P("layer", "blk")
    return jax.shard_map(
        on_device, mesh=mesh, in_specs=in_specs, out_specs=out_specs, check_vma=False
    )
```

profile of v0, /device:TPU:0, one launch (start us, length us, event | category | flops | bytes accessed | tf_op | source)
XLA Modules:
  0.0 88.4 jit_solution(17370040293893275652)
XLA Ops:
  0.0 0.0 copy-start
  0.0 0.7 convert_element_type.30
  0.7 0.0 copy-start.2
  0.7 0.0 copy-start.1
  0.7 15.9 %fusion.13 = f32[4096]{0:T(1024)S(1)} fusion(s32[4096]{0:T(1024)} %bitcast.33), kind=kOutput, calls=%fused_computation.18 | convolution fusion | flops 285339648 | bytes 32768 | tf_op jit(solution)/shard_map/dot_general | solution.py:21
  16.7 0.0 copy-done.2
  16.7 0.0 copy-done.1
  16.7 43.1 %fusion = f32[5,8192]{1,0:T(8,128)} fusion(s32[4096]{0:T(1024)S(1)} %bitcast.34, f32[5,4096]{1,0:T(8,128)S(1)} %fusion.36), kind=kOutput, calls=%fused_computation.1 | convolution fusion | flops 2046820352 | bytes 262144 | tf_op jit(solution)/shard_map/dot_general | solution.py:21
  59.8 7.3 %all-to-all-start = ((f32[5,8,1024]{2,0,1:T(8,128)}), f32[5,8,1024]{2,0,1:T(8,128)S(1)}, u32[]{:S(2)}, u32[]{:S(2)}) async-start(f32[5,8,1024]{2,0,1:T(8,128)} %bitcast.4), calls=%async_computation | async-start | bytes 524288 | tf_op jit(solution)/shard_map/all_to_all | solution.py:45
  68.5 7.6 %all-to-all-done = f32[5,8,1024]{2,0,1:T(8,128)S(1)} async-done(((f32[5,8,1024]{2,0,1:T(8,128)}), f32[5,8,1024]{2,0,1:T(8,128)S(1)}, u32[]{:S(2)}, u32[]{:S(2)}) %all-to-all-start) | async-done | bytes 163872 | tf_op jit(solution)/shard_map/all_to_all | solution.py:45
  76.1 0.0 copy-done
  76.1 1.4 %fusion.9 = f32[8192,10]{0,1:T(8,128)S(1)} fusion(f32[10,128]{1,0:T(8,128)S(1)} %copy-done, s32[8192]{0:T(1024)S(1)} %bitcast.30), kind=kOutput, calls=%fused_computation.14 | convolution fusion | flops 126877696 | bytes 365568 | tf_op jit(solution)/shard_map/dot_general | solution.py:21
  77.6 0.0 copy-start.3
  77.6 2.1 %fusion.6 = f32[4,8192]{1,0:T(4,128)S(1)} fusion(f32[4,8192]{1,0:T(4,128)S(1)} %bitcast.27, s32[8192]{0:T(1024)S(1)} %bitcast.31, f32[12,4,128]{2,1,0:T(4,128)} %param.8, s32[]{:T(128)S(6)} %select_n.16, s32[]{:T(128)S(6)} %select_n.14, f32[]{:T(128)S(6)} %sub.10, f32[]{:T(128)} %bitcast.25), kind=kOutput, calls=%fused_computation.10 | convolution fusion | flops 51480064 | bytes 299532 | tf_op jit(solution)/shard_map/dot_general | solution.py:21
  79.7 0.0 copy-done.3
  79.7 0.4 fusion.3
  80.1 2.0 %fusion.28 = (f32[128]{0:T(128)S(1)}, f32[4,128]{1,0:T(4,128)S(1)}) fusion(f32[4,8192]{1,0:T(4,128)S(1)} %fusion.3, s32[8192]{0:T(1024)S(1)} %bitcast.32), kind=kOutput, calls=%fused_computation.38 | convolution fusion | flops 51380608 | bytes 166400 | tf_op jit(solution)/shard_map/dot_general | solution.py:21
  82.1 5.7 %psum.7 = f32[128]{0:T(128)S(1)} all-reduce(f32[128]{0:T(128)S(1)} %get-tuple-element.5), channel_id=1, replica_groups=mesh['blk'=8,'layer'=4] {'layer'}, use_global_device_ids=true, to_apply=%region_2.3 | all-reduce | flops 128 | bytes 1024 | tf_op jit(solution)/shard_map/psum | solution.py:54
  87.8 0.6 broadcast_divide_fusion
  (6 shorter events, 0.1 us)
Async XLA Ops:
  0.0 76.1 %copy-start = (f32[10,128]{1,0:T(8,128)S(1)}, f32[10,128]{1,0:T(8,128)}, u32[]{:S(2)}) copy-start(f32[10,128]{1,0:T(8,128)} %param.9) | copy-start | bytes 15364
  0.7 15.9 %copy-start.2 = (s32[4096,1]{0,1:T(1,128)S(1)}, s32[4096,1]{0,1:T(1,128)}, u32[]{:S(2)}) copy-start(s32[4096,1]{0,1:T(1,128)} %param.12) | copy-start | bytes 49156
  0.7 16.0 %copy-start.1 = (f32[4,4096]{1,0:T(4,128)S(1)}, f32[4,4096]{1,0:T(4,128)}, u32[]{:S(2)}) copy-start(f32[4,4096]{1,0:T(4,128)} %param.11) | copy-start | bytes 196612
  59.8 16.2 %all-to-all-start = ((f32[5,8,1024]{2,0,1:T(8,128)}), f32[5,8,1024]{2,0,1:T(8,128)S(1)}, u32[]{:S(2)}, u32[]{:S(2)}) async-start(f32[5,8,1024]{2,0,1:T(8,128)} %bitcast.4), calls=%async_computation | async-start | bytes 524288 | tf_op jit(solution)/shard_map/all_to_all | solution.py:45
  77.6 2.1 %copy-start.3 = (f32[4,10]{1,0:T(4,128)S(1)}, f32[4,10]{1,0:T(4,128)}, u32[]{:S(2)}) copy-start(f32[4,10]{1,0:T(4,128)} %param.10) | copy-start | bytes 484
where the time goes:
time: 88.8 us; the launch traced here: 88.4 us
  matrix products  64.9 us (73%)
  waiting for transfers between devices  7.59 us (9%)
  starting transfers between devices  7.31 us (8%)
  blocking collectives  5.67 us (6%)
  other arithmetic  1.43 us (2%)
  between operations  1.42 us (2%)
    dot_general x5, matrix products, exact_dot(): return jnp.dot(left, right, precision=lax.Precision.HIGHEST)  64.5 us
    all_to_all x1, waiting for transfers between devices, on_device(): lax.all_to_all(buffer, 'blk', split_axis=1, concat_axis=1, tiled=True)  7.59 us
    all_to_all x1, starting transfers between devices, on_device(): lax.all_to_all(buffer, 'blk', split_axis=1, concat_axis=1, tiled=True)  7.31 us
    psum x1, blocking collectives, on_device(): total = lax.psum(jnp.sum(grid_sum, axis=0), 'layer')  5.67 us
  transfers between devices with their start and end apart: 1, of which 1 were waited for; matrix products, arithmetic and copies ran while one was open for 0% of the time, Pallas kernels for 0%

commit v1 on v0

v1 whole, which is shorter than its diff:
```python
import functools

import jax
import jax.numpy as jnp
from jax import lax
from jax.experimental import pallas as pl
from jax.experimental.pallas import tpu as pltpu
from jax.sharding import PartitionSpec as P

MESH = pl.DeviceIdType.MESH
CHUNK = 512


def local_sums(weight, owner, local, owners, cells):
    types, patches = weight.shape
    chunk = CHUNK if patches % CHUNK == 0 else patches
    row_owner = lax.broadcasted_iota(jnp.int32, (owners * types, chunk), 0) // types
    cell = lax.broadcasted_iota(jnp.int32, (cells, chunk), 0)
    total = None
    for start in range(0, patches, chunk):
        part = slice(start, start + chunk)
        w = weight[:, part]
        high = w.astype(jnp.bfloat16).astype(jnp.float32)
        low = w - high
        named = row_owner == owner[:, part]
        left = jnp.concatenate(
            [
                jnp.where(named, jnp.concatenate([piece] * owners, axis=0), 0.0)
                for piece in (high, low)
            ],
            axis=0,
        ).astype(jnp.bfloat16)
        table = jnp.where(cell == local[:, part], 1.0, 0.0).astype(jnp.bfloat16)
        product = lax.dot_general(
            left, table, (((1,), (1,)), ((), ())), preferred_element_type=jnp.float32
        )
        total = product if total is None else total + product
    return total[: owners * types] + total[owners * types :]


def kernel(
    n, m, leaf_hbm, soil_hbm, root_hbm, weight_hbm, owner_hbm, local_hbm, month_hbm, mix_hbm,
    out_ref, leaf, soil, root, weight, owner, local, month, mix,
    sums, pair, got_sums, got_pairs, load_sem, send_sem, recv_sem,
):
    blk, layer = lax.axis_index("blk"), lax.axis_index("layer")
    types, cells = out_ref.shape
    loads = [
        pltpu.make_async_copy(source, target, load_sem.at[i])
        for i, (source, target) in enumerate(
            (
                (weight_hbm, weight),
                (owner_hbm, owner),
                (local_hbm, local),
                (month_hbm, month),
                (mix_hbm, mix),
                (leaf_hbm, leaf),
                (soil_hbm, soil),
                (root_hbm, root),
            )
        )
    ]
    for load in loads:
        load.start()

    def device(step_blk, step_layer):
        return (lax.rem(blk + step_blk, n), lax.rem(layer + step_layer, m))

    steps = [(i, j) for i in range(n) for j in range(m) if i or j]
    barrier = pltpu.get_barrier_semaphore()
    for step in steps:
        pl.semaphore_signal(barrier, inc=1, device_id=device(*step), device_id_type=MESH)

    for load in loads[:3]:
        load.wait()
    partial = local_sums(weight, owner, local, n, cells)
    for i in range(n):
        sums[i] = partial[i * types : (i + 1) * types]
    for load in loads[3:]:
        load.wait()
    first = month[0]
    second = lax.rem(first + 1, leaf.shape[0])
    current = mix[0] * leaf[first] + (1.0 - mix[0]) * leaf[second]
    stress = root[:, 0:1] * soil[0:1, :]
    for i in range(1, soil.shape[0]):
        stress += root[:, i : i + 1] * soil[i : i + 1, :]
    effect = (1.0 - jnp.exp(-0.5 * current)) * stress
    own = sums[blk]
    pair[0] = own
    pair[1] = effect

    pl.semaphore_wait(barrier, len(steps))
    for i, j in reversed(steps):
        if i:
            source, target, k = (
                sums.at[lax.rem(blk + i, n)],
                got_sums.at[j * (n - 1) + i - 1],
                0,
            )
        else:
            source, target, k = pair, got_pairs.at[j - 1], 1
        pltpu.make_async_remote_copy(
            src_ref=source,
            dst_ref=target,
            send_sem=send_sem.at[k],
            recv_sem=recv_sem.at[k],
            device_id=device(i, j),
            device_id_type=MESH,
        ).start()
    pltpu.make_async_copy(got_sums, got_sums, recv_sem.at[0]).wait()
    pltpu.make_async_copy(got_pairs, got_pairs, recv_sem.at[1]).wait()

    mine, everyone = None, None
    for j in range(m):
        grid = own if j == 0 else got_pairs[j - 1, 0]
        for i in range(n - 1):
            grid = grid + got_sums[j * (n - 1) + i]
        grid = grid * (effect if j == 0 else got_pairs[j - 1, 1])
        if j == 0:
            mine = grid
            everyone = grid
        else:
            everyone = everyone + grid
    out_ref[...] = mine / (1.0 + jnp.sum(everyone, axis=0, keepdims=True))
    pltpu.make_async_copy(got_sums, got_sums, send_sem.at[0]).wait()
    pltpu.make_async_copy(got_pairs, got_pairs, send_sem.at[1]).wait()


def on_device(
    leaf_area, soil_water, root_share, patch_weight, patch_owner, patch_local, month, mix
):
    n, m = lax.axis_size("blk"), lax.axis_size("layer")
    months, types, cells = leaf_area.shape
    patches = patch_local.shape[0]
    owner = patch_owner.reshape(1, patches)
    local = patch_local.reshape(1, patches)
    f32, i32 = jnp.float32, jnp.int32
    return pl.pallas_call(
        functools.partial(kernel, n, m),
        out_shape=jax.ShapeDtypeStruct((types, cells), f32),
        in_specs=[pl.BlockSpec(memory_space=pl.ANY)] * 8,
        out_specs=pl.BlockSpec(memory_space=pltpu.VMEM),
        scratch_shapes=[
            pltpu.VMEM(leaf_area.shape, f32),
            pltpu.VMEM(soil_water.shape, f32),
            pltpu.VMEM(root_share.shape, f32),
            pltpu.VMEM(patch_weight.shape, f32),
            pltpu.VMEM(owner.shape, i32),
            pltpu.VMEM(local.shape, i32),
            pltpu.SMEM(month.shape, i32),
            pltpu.SMEM(mix.shape, f32),
            pltpu.VMEM((n, types, cells), f32),
            pltpu.VMEM((2, types, cells), f32),
            pltpu.VMEM((m * (n - 1), types, cells), f32),
            pltpu.VMEM((m - 1, 2, types, cells), f32),
            pltpu.SemaphoreType.DMA((8,)),
            pltpu.SemaphoreType.DMA((2,)),
            pltpu.SemaphoreType.DMA((2,)),
        ],
        compiler_params=pltpu.CompilerParams(collective_id=0, has_side_effects=True),
    )(leaf_area, soil_water, root_share, patch_weight, owner, local, month, mix)


def solution(mesh):
    in_specs = (
        P(None, "layer", "blk"),
        P(None, "blk"),
        P("layer", None),
        P("layer", "blk"),
        P("blk", None),
        P("blk"),
        P(),
        P(),
    )
    out_specs = P("layer", "blk")
    return jax.shard_map(
        on_device, mesh=mesh, in_specs=in_specs, out_specs=out_specs, check_vma=False
    )
```

time: 88.8 us -> 13.9 us (0.16)
  matrix products: 64.9 us -> 0 us
  Pallas kernels: 0 us -> 11.2 us
  waiting for transfers between devices: 7.59 us -> 0 us
  starting transfers between devices: 7.31 us -> 0 us
  blocking collectives: 5.67 us -> 0 us
  other arithmetic: 1.43 us -> 0 us
  local copies, waits for them, and re-layouts: 0.04 us -> 1.26 us
    dot_general x6 -> x0, matrix products: 64.9 us -> none  [the longest x5 64.5 us: exact_dot(): return jnp.dot(left, right, precision=lax.Precision.HIGHEST)]
    pallas_call x0 -> x1, Pallas kernels: none -> 11.2 us  [on_device(): pl.pallas_call(functools.partial(kernel, n, m), out_shape=jax.ShapeDtypeS...]
    all_to_all x1 -> x0, waiting for transfers between devices: 7.59 us -> none  [on_device(): lax.all_to_all(buffer, 'blk', split_axis=1, concat_axis=1, tiled=True)]
    all_to_all x1 -> x0, starting transfers between devices: 7.31 us -> none  [on_device(): lax.all_to_all(buffer, 'blk', split_axis=1, concat_axis=1, tiled=True)]
    psum x1 -> x0, blocking collectives: 5.67 us -> none  [on_device(): total = lax.psum(jnp.sum(grid_sum, axis=0), 'layer')]
    unnamed x8 -> x1, local copies, waits for them, and re-layouts: 0.02 us -> 1.26 us
  transfers between devices with their start and end apart: 1 -> 0, of which waited for: 1 -> 0; matrix products, arithmetic and copies ran while one was open for 0% -> 0% of each run, Pallas kernels for 0% -> 0%
where the time goes in v1:
time: 13.9 us; the launch traced here: 13.7 us
  Pallas kernels  11.2 us (81%)
  between operations  1.3 us (9%)
  local copies, waits for them, and re-layouts  1.26 us (9%)
    pallas_call x1, Pallas kernels, on_device(): pl.pallas_call(functools.partial(kernel, n, m), out_shape=jax.ShapeDtypeS...  11.2 us
    unnamed x1, local copies, waits for them, and re-layouts  1.26 us

profile of v1, /device:TPU:0, one launch (start us, length us, event | category | flops | bytes accessed | tf_op | source)
XLA Modules:
  0.0 13.7 jit_solution(9641128658111135365)
XLA Ops:
  1.3 11.2 %shard_map.82 = f32[4,128]{1,0:T(4,128)} custom-call(f32[12,4,128]{2,1,0:T(4,128)} %leaf_hbm.1, f32[10,128]{1,0:T(8,128)} %soil_hbm.1, f32[4,10]{1,0:T(4,128)} %root_hbm.1, f32[4,4096]{1,0:T(4,128)} %weight_hbm.1, s32[1,4096]{1,0:T(1,128)} %bitcast.2, s32[1,4096]{1,0:T(1,128)} %bitcast.3, s32[1]{0:T(128)S(6)} %copy.10.month_hbm, f32[1]{0:T(128)S(6)} %copy.11.mix_hbm), custom_call_target="tpu_custom_call" | custom-call | tf_op jit(solution)/shard_map/pallas_call | solution.py:138
  12.5 1.3 %copy.12 = f32[4,128]{1,0:T(4,128)} copy(f32[4,128]{1,0:T(4,128)} %shard_map.82) | data formatting | bytes 4096

commit v2 on v1

--- a/solution.py
+++ b/solution.py
@@ -137,7 +137,7 @@
     f32, i32 = jnp.float32, jnp.int32
     return pl.pallas_call(
         functools.partial(kernel, n, m),
-        out_shape=jax.ShapeDtypeStruct((types, cells), f32),
+        out_shape=pltpu.VMEM((types, cells), f32),
         in_specs=[pl.BlockSpec(memory_space=pl.ANY)] * 8,
         out_specs=pl.BlockSpec(memory_space=pltpu.VMEM),
         scratch_shapes=[

time: 13.9 us -> 12.6 us (0.906)
  local copies, waits for them, and re-layouts: 1.26 us -> 0.58 us
  Pallas kernels: 11.2 us -> 10.6 us
    unnamed x1, local copies, waits for them, and re-layouts: 1.26 us -> 0.58 us
    pallas_call x1, Pallas kernels: 11.2 us -> 10.6 us  [on_device(): pl.pallas_call(functools.partial(kernel, n, m), out_shape=pltpu.VMEM((typ...]
where the time goes in v2:
time: 12.6 us; the launch traced here: 12.5 us
  Pallas kernels  10.6 us (84%)
  between operations  1.3 us (10%)
  local copies, waits for them, and re-layouts  0.58 us (5%)
    pallas_call x1, Pallas kernels, on_device(): pl.pallas_call(functools.partial(kernel, n, m), out_shape=pltpu.VMEM((typ...  10.6 us
    unnamed x1, local copies, waits for them, and re-layouts  0.58 us

profile of v2, /device:TPU:0, one launch (start us, length us, event | category | flops | bytes accessed | tf_op | source)
XLA Modules:
  0.0 12.5 jit_solution(7738650130451298089)
XLA Ops:
  1.3 10.6 %shard_map.82 = f32[4,128]{1,0:T(4,128)S(1)} custom-call(f32[12,4,128]{2,1,0:T(4,128)} %leaf_hbm.1, f32[10,128]{1,0:T(8,128)} %soil_hbm.1, f32[4,10]{1,0:T(4,128)} %root_hbm.1, f32[4,4096]{1,0:T(4,128)} %weight_hbm.1, s32[1,4096]{1,0:T(1,128)} %bitcast.2, s32[1,4096]{1,0:T(1,128)} %bitcast.3, s32[1]{0:T(128)S(6)} %copy.11.month_hbm, f32[1]{0:T(128)S(6)} %copy.12.mix_hbm), custom_call_target="tpu_custom_call" | custom-call | tf_op jit(solution)/shard_map/pallas_call | solution.py:138
  11.9 0.6 %copy.10 = f32[4,128]{1,0:T(4,128)} copy(f32[4,128]{1,0:T(4,128)S(1)} %shard_map.82) | data formatting | bytes 4096

commit v3 on v2

--- a/solution.py
+++ b/solution.py
@@ -90,7 +90,7 @@
     pair[1] = effect
 
     pl.semaphore_wait(barrier, len(steps))
-    for i, j in reversed(steps):
+    for i, j in steps:
         if i:
             source, target, k = (
                 sums.at[lax.rem(blk + i, n)],

time: 12.6 us -> 12.2 us (0.968)
  Pallas kernels: 10.6 us -> 10.2 us
    pallas_call x1, Pallas kernels: 10.6 us -> 10.2 us  [on_device(): pl.pallas_call(functools.partial(kernel, n, m), out_shape=pltpu.VMEM((typ...]
where the time goes in v3:
time: 12.2 us; the launch traced here: 12 us
  Pallas kernels  10.2 us (84%)
  between operations  1.3 us (11%)
  local copies, waits for them, and re-layouts  0.58 us (5%)
    pallas_call x1, Pallas kernels, on_device(): pl.pallas_call(functools.partial(kernel, n, m), out_shape=pltpu.VMEM((typ...  10.2 us
    unnamed x1, local copies, waits for them, and re-layouts  0.58 us

profile of v3, /device:TPU:0, one launch (start us, length us, event | category | flops | bytes accessed | tf_op | source)
XLA Modules:
  0.0 12.0 jit_solution(5810225006042652536)
XLA Ops:
  1.3 10.2 %shard_map.82 = f32[4,128]{1,0:T(4,128)S(1)} custom-call(f32[12,4,128]{2,1,0:T(4,128)} %leaf_hbm.1, f32[10,128]{1,0:T(8,128)} %soil_hbm.1, f32[4,10]{1,0:T(4,128)} %root_hbm.1, f32[4,4096]{1,0:T(4,128)} %weight_hbm.1, s32[1,4096]{1,0:T(1,128)} %bitcast.2, s32[1,4096]{1,0:T(1,128)} %bitcast.3, s32[1]{0:T(128)S(6)} %copy.11.month_hbm, f32[1]{0:T(128)S(6)} %copy.12.mix_hbm), custom_call_target="tpu_custom_call" | custom-call | tf_op jit(solution)/shard_map/pallas_call | solution.py:138
  11.5 0.6 %copy.10 = f32[4,128]{1,0:T(4,128)} copy(f32[4,128]{1,0:T(4,128)S(1)} %shard_map.82) | data formatting | bytes 4096
